TPU v7x, 256 devices: a whole 4x4x8 slice. The times are simulated.
256 devices in a mesh: row: 16 (over z, y_hi), col: 8 (over x, core), depth: 2 (over y_lo).
Axes of the slice: x: 4, y: 4 (y_hi: 2, y_lo: 2; y = y_hi * 2 + y_lo), z: 8, core: 2. Of those that a mesh axis runs over, the one named last changes fastest.
Arguments:
- heads_concat: bfloat16 [8192, 16384], P('row', ('depth', 'col')), may hold values from -6 to 6
- w_out: bfloat16 [16384, 7168], P(('depth', 'row'), 'col'), may hold values from -0.046875 to 0.046875
Outputs:
- projected: bfloat16 [8192, 7168], P('row', ('col', 'depth'))
All inputs are finite; a program needn't handle non-finite values.
Results may differ from a plain program's by a relative error of at most 0.001.
Values may be sent and summed in bfloat16 or wider, within the bound.
A program may use at most 128 MiB of HBM per device.

v0:
```python
import jax
import jax.numpy as jnp
from jax import lax
from jax.sharding import PartitionSpec as P


def from_everyone(array, axis):
    copies = jnp.broadcast_to(array, (lax.axis_size(axis), *array.shape))
    return lax.all_to_all(copies, axis, split_axis=0, concat_axis=0, tiled=True)


def joined_along(tiles, dim):
    tiles = jnp.moveaxis(tiles, 0, dim)
    shape = tiles.shape
    return tiles.reshape(*shape[:dim], shape[dim] * shape[dim + 1], *shape[dim + 2 :])


def collect(array, axis, dim):
    tiles = from_everyone(array, axis)
    return joined_along(tiles, dim)


def in_blocks(array, dim, size):
    shape = array.shape
    tiles = array.reshape(*shape[:dim], size, shape[dim] // size, *shape[dim + 1 :])
    return jnp.moveaxis(tiles, dim, 0)


def summed_on_arrival(array, axis, dim):
    size = lax.axis_size(axis)
    tiles = lax.all_to_all(in_blocks(array, dim, size), axis, 0, 0, tiled=True)
    return jnp.sum(tiles, axis=0)


def per_device(heads_concat, w_out):
    weight_half = lax.all_gather(w_out, "row", axis=0, tiled=True)
    partial_sum = jnp.dot(
        collect(heads_concat, "col", 1), weight_half, preferred_element_type=jnp.float32
    )
    summed = summed_on_arrival(partial_sum, "depth", 1)
    return summed.astype(jnp.bfloat16)


def solution(mesh):
    return jax.shard_map(
        per_device,
        mesh=mesh,
        in_specs=(P("row", ("depth", "col")), P(("depth", "row"), "col")),
        out_specs=P("row", ("col", "depth")),
        check_vma=False,
    )
```

profile of v0, /device:TPU:2, one launch (start us, length us, event | category | flops | bytes accessed | tf_op | source)
XLA Modules:
  0.0 278.8 jit_solution(3857132418449797120)
XLA Ops:
  6.5 0.0 all-gather.2.cloned.1.call-start
  6.5 0.7 all-gather.2.cloned.1.call-update
  7.3 2.3 broadcast_in_dim.3
  9.5 100.0 %all_to_all.10 = bf16[8,512,1024]{2,1,0:T(8,128)(2,1)} all-to-all(bf16[8,512,1024]{2,1,0:T(8,128)(2,1)S(1)} %broadcast_in_dim.3), channel_id=1, replica_groups=mesh['row'=16,'col'=8,'depth'=2] {'col'}, dimensions={0} | all-to-all | bytes 16777216 | tf_op jit(solution)/shard_map/all_to_all | solution.py:9
  109.5 11.4 %copy.4 = bf16[512,8,1024]{2,1,0:T(8,128)(2,1)} copy(bf16[512,8,1024]{2,0,1:T(8,128)(2,1)} %bitcast.7) | data formatting | bytes 16777216 | tf_op jit(solution)/shard_map/transpose | solution.py:13
  120.9 13.5 %reshape.6 = bf16[512,8192,1]{1,0,2:T(8,128)(2,1)} reshape(bf16[512,8,1024]{2,1,0:T(8,128)(2,1)} %copy.4) | data formatting | bytes 16777216 | tf_op jit(solution)/shard_map/reshape | solution.py:15
  134.4 79.6 %all-gather.2.cloned.1.call-done = bf16[8192,896]{1,0:T(8,128)(2,1)} async-done(((bf16[512,896]{1,0:T(8,128)(2,1)}), bf16[8192,896]{1,0:T(8,128)(2,1)}) %all-gather.2.cloned.1.call-update) | async-done | bytes 14680080 | tf_op jit(solution)/shard_map/all_gather | solution.py:36
  214.0 19.4 %copy.5 = bf16[896,8192]{1,0:T(8,128)(2,1)} copy(bf16[896,8192]{0,1:T(8,128)(2,1)} %bitcast.8) | data formatting | bytes 29360128 | tf_op jit(solution)/shard_map/dot_general | solution.py:37
  233.4 13.5 %convolution_bitcast_fusion = f32[2,512,448]{1,2,0:T(8,128)S(1)} fusion(bf16[512,8192,1]{1,0,2:T(8,128)(2,1)} %reshape.6, bf16[2,448,8192]{2,1,0:T(8,128)(2,1)} %bitcast.9), kind=kOutput, calls=%fused_computation | convolution fusion | flops 7516192768 | bytes 24903680 | tf_op jit(solution)/shard_map/dot_general | solution.py:37
  246.9 24.1 %all_to_all.11 = f32[2,512,448]{1,2,0:T(8,128)S(1)} all-to-all(f32[2,512,448]{1,2,0:T(8,128)S(1)} %convolution_bitcast_fusion), channel_id=1, replica_groups=mesh['row'=16,'col'=8,'depth'=2] {'depth'}, dimensions={0} | all-to-all | bytes 3670016 | tf_op jit(solution)/shard_map/all_to_all | solution.py:31
  271.0 1.0 reduce_sum.9
Async XLA Ops:
  6.5 207.5 %all-gather.2.cloned.1.call-start = ((), (), s32[]{:S(2)}) async-start(), calls=%async_computation.2 | async-start | bytes 15597568 | tf_op jit(solution)/shard_map/all_gather | solution.py:36
Sparse Core Ops, SparseCore 0:
  9.9 204.0 all-gather.1
where the time goes:
time: 280 us; the launch traced here: 279 us
  blocking collectives  124 us (44%)
  waiting for transfers between devices  80.3 us (29%)
  local copies, waits for them, and re-layouts  46.5 us (17%)
  matrix products  13.5 us (5%)
  between operations  13.4 us (5%)
    all_to_all x1, blocking collectives, from_everyone(): return lax.all_to_all(copies, axis, split_axis=0, concat_axis=0, tiled=True)  100 us
    all_gather x1, waiting for transfers between devices, per_device(): weight_half = lax.all_gather(w_out, 'row', axis=0, tiled=True)  79.6 us
    all_to_all x1, blocking collectives, summed_on_arrival(): tiles = lax.all_to_all(in_blocks(array, dim, size), axis, 0, 0, tiled=True)  24.1 us
    dot_general x1, local copies, waits for them, and re-layouts, per_device(): jnp.dot(collect(heads_concat, 'col', 1), weight_half, preferred_element_t...  19.4 us
    reshape x1, local copies, waits for them, and re-layouts, joined_along(): tiles.reshape(*shape[:dim], shape[dim] * shape[dim + 1], *shape[dim + 2:])  13.5 us
    dot_general x1, matrix products, per_device(): jnp.dot(collect(heads_concat, 'col', 1), weight_half, preferred_element_t...  13.5 us
    transpose x1, local copies, waits for them, and re-layouts, joined_along(): tiles = jnp.moveaxis(tiles, 0, dim)  11.4 us
  transfers between devices with their start and end apart: 1, of which 1 were waited for; matrix products, arithmetic and copies ran while one was open for 10% of the time, Pallas kernels for 0%

commit v1 on v0

--- a/solution.py
+++ b/solution.py
@@ -33,7 +33,10 @@
 
 
 def per_device(heads_concat, w_out):
-    weight_half = lax.all_gather(w_out, "row", axis=0, tiled=True)
+    count = lax.axis_size("row")
+    blocks = jnp.stack([w_out for _ in range(count)])
+    blocks = lax.all_to_all(blocks, "row", split_axis=0, concat_axis=0)
+    weight_half = jnp.concatenate(blocks, axis=0)
     partial_sum = jnp.dot(
         collect(heads_concat, "col", 1), weight_half, preferred_element_type=jnp.float32
     )

time: 280 us -> 537 us (1.92)
  waiting for transfers between devices: 80.3 us -> 402 us
  blocking collectives: 124 us -> 23.7 us
  local copies, waits for them, and re-layouts: 46.5 us -> 76.8 us
  starting transfers between devices: 0.01 us -> 16.8 us
  between operations: 13.4 us -> 0.03 us
    all_to_all x0 -> x2, waiting for transfers between devices: none -> 402 us  [the longest x1 310 us: per_device(): blocks = lax.all_to_all(blocks, 'row', split_axis=0, concat_axis=0)]
    all_to_all x1 -> x0, blocking collectives: 100 us -> none  [from_everyone(): return lax.all_to_all(copies, axis, split_axis=0, concat_axis=0, tiled=True)]
    all_gather x1 -> x0, waiting for transfers between devices: 79.6 us -> none  [per_device(): weight_half = lax.all_gather(w_out, 'row', axis=0, tiled=True)]
    all_to_all x0 -> x1, local copies, waits for them, and re-layouts: none -> 19.9 us  [per_device(): blocks = lax.all_to_all(blocks, 'row', split_axis=0, concat_axis=0)]
    all_to_all x0 -> x2, starting transfers between devices: none -> 16.8 us  [the longest x1 9.54 us: per_device(): blocks = lax.all_to_all(blocks, 'row', split_axis=0, concat_axis=0)]
    another operation x0 -> x1, local copies, waits for them, and re-layouts: none -> 6.6 us  [per_device(): blocks = jnp.stack([w_out for _ in range(count)])]
  transfers between devices with their start and end apart: 1 -> 2, of which waited for: 1 -> 2; matrix products, arithmetic and copies ran while one was open for 10% -> 5% of each run, Pallas kernels for 0% -> 0%
where the time goes in v1:
time: 537 us; the launch traced here: 534 us
  waiting for transfers between devices  402 us (75%)
  local copies, waits for them, and re-layouts  76.8 us (14%)
  blocking collectives  23.7 us (4%)
  starting transfers between devices  16.8 us (3%)
  matrix products  13.5 us (3%)
    all_to_all x1, waiting for transfers between devices, per_device(): blocks = lax.all_to_all(blocks, 'row', split_axis=0, concat_axis=0)  310 us
    all_to_all x1, waiting for transfers between devices, from_everyone(): return lax.all_to_all(copies, axis, split_axis=0, concat_axis=0, tiled=True)  92.7 us
    all_to_all x1, blocking collectives, summed_on_arrival(): tiles = lax.all_to_all(in_blocks(array, dim, size), axis, 0, 0, tiled=True)  23.7 us
    all_to_all x1, local copies, waits for them, and re-layouts, per_device(): blocks = lax.all_to_all(blocks, 'row', split_axis=0, concat_axis=0)  19.9 us
    dot_general x1, local copies, waits for them, and re-layouts, per_device(): jnp.dot(collect(heads_concat, 'col', 1), weight_half, preferred_element_t...  19.4 us
    reshape x1, local copies, waits for them, and re-layouts, joined_along(): tiles.reshape(*shape[:dim], shape[dim] * shape[dim + 1], *shape[dim + 2:])  13.5 us
    dot_general x1, matrix products, per_device(): jnp.dot(collect(heads_concat, 'col', 1), weight_half, preferred_element_t...  13.5 us
    transpose x1, local copies, waits for them, and re-layouts, joined_along(): tiles = jnp.moveaxis(tiles, 0, dim)  11.3 us
  transfers between devices with their start and end apart: 2, of which 2 were waited for; matrix products, arithmetic and copies ran while one was open for 5% of the time, Pallas kernels for 0%

profile of v1, /device:TPU:2, one launch (start us, length us, event | category | flops | bytes accessed | tf_op | source)
XLA Modules:
  0.0 534.2 jit_solution(7700244152493029967)
XLA Ops:
  0.0 5.5 %broadcast_in_dim.3 = bf16[8,512,1024]{2,1,0:T(8,128)(2,1)} broadcast(bf16[512,1024]{1,0:T(8,128)(2,1)} %param.2), dimensions={1,2} | broadcast | bytes 9437184 | tf_op jit(solution)/shard_map/broadcast_in_dim | solution.py:8
  5.5 0.0 copy-start
  5.5 7.3 %all-to-all-start = ((bf16[8,512,1024]{2,1,0:T(8,128)(2,1)}), bf16[8,512,1024]{2,1,0:T(8,128)(2,1)}, u32[]{:S(2)}, u32[]{:S(2)}) async-start(bf16[8,512,1024]{2,1,0:T(8,128)(2,1)} %broadcast_in_dim.3), calls=%async_computation | async-start | bytes 16777216 | tf_op jit(solution)/shard_map/all_to_all | solution.py:9
  12.8 0.0 copy-done
  12.8 0.5 copy.7
  13.3 92.7 %all-to-all-done = bf16[8,512,1024]{2,1,0:T(8,128)(2,1)} async-done(((bf16[8,512,1024]{2,1,0:T(8,128)(2,1)}), bf16[8,512,1024]{2,1,0:T(8,128)(2,1)}, u32[]{:S(2)}, u32[]{:S(2)}) %all-to-all-start) | async-done | bytes 8388640 | tf_op jit(solution)/shard_map/all_to_all | solution.py:9
  106.1 6.6 %stack.2 = bf16[16,512,896]{1,2,0:T(8,128)(2,1)} broadcast(bf16[512,896]{0,1:T(8,128)(2,1)S(1)} %copy.7), dimensions={1,2} | broadcast | bytes 15597568 | tf_op jit(solution)/shard_map/stack | solution.py:37
  112.7 9.5 %all-to-all-start.1 = ((bf16[16,512,896]{1,2,0:T(8,128)(2,1)}), bf16[16,512,896]{1,2,0:T(8,128)(2,1)}, u32[]{:S(2)}, u32[]{:S(2)}) async-start(bf16[16,512,896]{1,2,0:T(8,128)(2,1)} %stack.2), calls=%async_computation.1 | async-start | bytes 29360128 | tf_op jit(solution)/shard_map/all_to_all | solution.py:38
  122.2 11.3 %copy.6 = bf16[512,8,1024]{2,1,0:T(8,128)(2,1)} copy(bf16[512,8,1024]{2,0,1:T(8,128)(2,1)} %bitcast) | data formatting | bytes 16777216 | tf_op jit(solution)/shard_map/transpose | solution.py:13
  133.5 13.5 %reshape.12 = bf16[512,8192,1]{1,0,2:T(8,128)(2,1)} reshape(bf16[512,8,1024]{2,1,0:T(8,128)(2,1)} %copy.6) | data formatting | bytes 16777216 | tf_op jit(solution)/shard_map/reshape | solution.py:15
  147.0 309.8 %all-to-all-done.1 = bf16[16,512,896]{1,2,0:T(8,128)(2,1)} async-done(((bf16[16,512,896]{1,2,0:T(8,128)(2,1)}), bf16[16,512,896]{1,2,0:T(8,128)(2,1)}, u32[]{:S(2)}, u32[]{:S(2)}) %all-to-all-start.1) | async-done | bytes 14680096 | tf_op jit(solution)/shard_map/all_to_all | solution.py:38
  456.7 19.9 %copy.8 = bf16[16,512,896]{2,1,0:T(8,128)(2,1)} copy(bf16[16,512,896]{1,2,0:T(8,128)(2,1)} %all-to-all-done.1) | data formatting | bytes 29360128 | tf_op jit(solution)/shard_map/all_to_all | solution.py:38
  476.6 19.4 %copy.9 = bf16[896,8192]{1,0:T(8,128)(2,1)} copy(bf16[896,8192]{0,1:T(8,128)(2,1)} %bitcast.9) | data formatting | bytes 29360128 | tf_op jit(solution)/shard_map/dot_general | solution.py:40
  496.1 13.5 %convolution_bitcast_fusion = f32[2,512,448]{1,2,0:T(8,128)S(1)} fusion(bf16[512,8192,1]{1,0,2:T(8,128)(2,1)} %reshape.12, bf16[2,448,8192]{2,1,0:T(8,128)(2,1)} %bitcast.10), kind=kOutput, calls=%fused_computation | convolution fusion | flops 7516192768 | bytes 24903680 | tf_op jit(solution)/shard_map/dot_general | solution.py:40
  509.5 23.7 %all_to_all.15 = f32[2,512,448]{1,2,0:T(8,128)S(1)} all-to-all(f32[2,512,448]{1,2,0:T(8,128)S(1)} %convolution_bitcast_fusion), channel_id=1, replica_groups=mesh['row'=16,'col'=8,'depth'=2] {'depth'}, dimensions={0} | all-to-all | bytes 3670016 | tf_op jit(solution)/shard_map/all_to_all | solution.py:31
  533.2 1.0 reduce_sum.9
Async XLA Ops:
  5.5 7.3 %copy-start = (bf16[512,896]{1,0:T(8,128)(2,1)S(1)}, bf16[512,896]{1,0:T(8,128)(2,1)}, u32[]{:S(2)}) copy-start(bf16[512,896]{1,0:T(8,128)(2,1)} %param.3) | copy-start | bytes 2752516
  5.5 100.5 %all-to-all-start = ((bf16[8,512,1024]{2,1,0:T(8,128)(2,1)}), bf16[8,512,1024]{2,1,0:T(8,128)(2,1)}, u32[]{:S(2)}, u32[]{:S(2)}) async-start(bf16[8,512,1024]{2,1,0:T(8,128)(2,1)} %broadcast_in_dim.3), calls=%async_computation | async-start | bytes 16777216 | tf_op jit(solution)/shard_map/all_to_all | solution.py:9
  112.7 344.1 %all-to-all-start.1 = ((bf16[16,512,896]{1,2,0:T(8,128)(2,1)}), bf16[16,512,896]{1,2,0:T(8,128)(2,1)}, u32[]{:S(2)}, u32[]{:S(2)}) async-start(bf16[16,512,896]{1,2,0:T(8,128)(2,1)} %stack.2), calls=%async_computation.1 | async-start | bytes 29360128 | tf_op jit(solution)/shard_map/all_to_all | solution.py:38
